TPU v7x, 256 devices: a whole 4x4x8 slice. The times are simulated.
256 devices in a mesh: gz: 64 (over z, x, core), col: 4 (over y).
Axes of the slice: x: 4, y: 4, z: 8, core: 2. Of those that a mesh axis runs over, the one named last changes fastest.
Arguments:
- source: float32 [4096, 2048], P('gz', 'col'), may hold values from -6 to 6
- z_vectors: float32 [4096, 4096], P('gz', 'col'), may hold values from -0.25 to 0.25
- x_vectors: float32 [4, 4], replicated, may hold values from -3 to 3
- y_vectors: float32 [512, 512], replicated, may hold values from -0.25 to 0.25
- z_values: float32 [4096], replicated, may hold values from 0.1 to 3
- x_values: float32 [4], replicated, may hold values from 0.1 to 3
- y_values: float32 [512], replicated, may hold values from 0.1 to 3
Outputs:
- solution: float32 [4096, 2048], P('gz', 'col')
All inputs are finite; a program needn't handle non-finite values.
Results may differ from a plain program's by a relative error of at most 0.000092.
Values sent between devices are 32-bit elements; how exact they have to be, the bound alone decides.
A program may use at most 64 MiB of HBM per device.

v0:
```python
import jax
import jax.numpy as jnp
from jax import lax
from jax.sharding import Mesh
from jax.sharding import PartitionSpec as P

GZ = ("gz_0", "gz_1", "gz_2")


exact_mode = lax.Precision.HIGHEST


def in_order(pieces, dim):
    shape = list(pieces.shape[1:])
    shape[dim] *= pieces.shape[0]
    return jnp.moveaxis(pieces, 0, dim).reshape(shape)


def sent_to_all(value, axis):
    devices = lax.axis_size(axis)
    return lax.all_to_all(
        jnp.broadcast_to(value[None], (devices, *value.shape)), axis, 0, 0, tiled=True
    )


def gather_directly(value, axis, dim):
    return in_order(sent_to_all(value, axis), dim)


def own_rows(subtotal, axes):
    for axis in axes:
        subtotal = lax.psum_scatter(subtotal, axis, scatter_dimension=0, tiled=True)
    return subtotal


def cut_along(value, dim, devices):
    shape = value.shape
    pieces = value.reshape(*shape[:dim], devices, shape[dim] // devices, *shape[dim + 1 :])
    return jnp.moveaxis(pieces, dim, 0)


def sum_at_owner(value, axis, dim):
    devices = lax.axis_size(axis)
    pieces = lax.all_to_all(cut_along(value, dim, devices), axis, 0, 0, tiled=True)
    return jnp.sum(pieces, axis=0)


def lead_product(left_side, right_side):
    return lax.dot_general(
        left_side,
        right_side,
        (((0,), (0,)), ((), ())),
        precision=exact_mode,
        preferred_element_type=jnp.float32,
    )


def shards(source, z_vectors, x_vectors, y_vectors, z_values, x_values, y_values):
    z_rows = source.shape[0]
    width_y = y_vectors.shape[0]
    width_x = x_vectors.shape[0]
    x_lines = source.shape[1] // width_y
    column = lax.axis_index("col")
    row_block = lax.axis_index(GZ)
    along_y = jnp.dot(source, y_vectors, precision=exact_mode, preferred_element_type=jnp.float32)
    planes = gather_directly(along_y, "col", 1)
    modal_full = jnp.einsum(
        "zxj,xi->zij", planes.reshape(z_rows, width_x, width_y), x_vectors, precision=exact_mode
    )
    modal_full = modal_full.reshape(z_rows, width_x * width_y)
    part_rows = z_rows // lax.axis_size("col")
    coeffs = own_rows(lead_product(z_vectors, modal_full), GZ)
    mode_start = column * z_vectors.shape[1] + row_block * part_rows
    z_part = lax.dynamic_slice_in_dim(z_values, mode_start, part_rows, 0)
    divisor = z_part[:, None, None] + x_values[None, :, None] + y_values[None, None, :]
    scaled = (coeffs.reshape(part_rows, width_x, width_y) / divisor).reshape(
        part_rows, width_x * width_y
    )
    back_z = jnp.dot(
        z_vectors,
        lax.all_gather(scaled, GZ, axis=0, tiled=True),
        precision=exact_mode,
        preferred_element_type=jnp.float32,
    )
    spread_x = jnp.einsum(
        "zij,xi->zxj", back_z.reshape(z_rows, width_x, width_y), x_vectors, precision=exact_mode
    )
    summed = sum_at_owner(spread_x.reshape(z_rows, width_x * width_y), "col", 1)
    back_x = summed.reshape(z_rows, x_lines, width_y)
    solution = lax.dot_general(
        back_x.reshape(z_rows * x_lines, width_y),
        y_vectors,
        (((1,), (1,)), ((), ())),
        precision=exact_mode,
        preferred_element_type=jnp.float32,
    )
    return solution


def solution(mesh):
    torus = Mesh(mesh.devices.reshape(8, 4, 2, mesh.shape["col"]), ("gz_0", "gz_1", "gz_2", "col"))
    return jax.shard_map(
        shards,
        mesh=torus,
        in_specs=(P(GZ, "col"), P(GZ, "col"), P(), P(), P(), P(), P()),
        out_specs=P(GZ, "col"),
        check_vma=False,
    )
```

profile of v0, /device:TPU:1, one launch (start us, length us, event | category | flops | bytes accessed | tf_op | source)
XLA Modules:
  0.0 293.1 jit_solution(16918401710747406262)
XLA Ops:
  6.5 0.0 copy-start
  6.5 1.2 copy-done
  7.8 1.7 fusion.7
  9.4 0.1 broadcast_in_dim.2
  9.5 13.4 %all_to_all.10 = f32[4,64,512]{2,1,0:T(8,128)S(1)} all-to-all(f32[4,64,512]{2,1,0:T(8,128)S(1)} %broadcast_in_dim.2), channel_id=1, replica_groups=mesh['gz_0'=8,'gz_1'=4,'gz_2'=2,'col'=4] {'col'}, dimensions={0} | all-to-all | bytes 1048576 | tf_op jit(solution)/shard_map/all_to_all | solution.py:21
  22.9 2.0 fusion.1
  24.9 0.2 copy.19
  25.1 10.0 %convolution_bitcast_fusion = f32[1024,2048]{0,1:T(8,128)} fusion(f32[64,2048]{1,0:T(8,128)S(1)} %bitcast.37, f32[64,1024]{1,0:T(8,128)} %param.8), kind=kOutput, calls=%fused_computation | convolution fusion | flops 1610612736 | bytes 9175040 | tf_op jit(solution)/shard_map/dot_general | solution.py:49
  35.1 0.0 reduce-scatter.8.cloned.1.call-update
  35.1 0.0 reduce-scatter.10.cloned.1.call-start
  35.2 97.1 %reduce-scatter.8.cloned.1.call-done = f32[128,2048]{0,1:T(8,128)} async-done(((f32[1024,2048]{0,1:T(8,128)}), f32[128,2048]{0,1:T(8,128)}) %reduce-scatter.8.cloned.1.call-update) | async-done | bytes 1048592 | tf_op jit(solution)/shard_map/reduce_scatter | solution.py:32
  132.2 2.5 copy.15
  134.8 0.0 reduce-scatter.10.cloned.1.call-update
  134.8 0.0 reduce-scatter.12.cloned.1.call-start
  134.8 23.6 %reduce-scatter.10.cloned.1.call-done = f32[32,2048]{1,0:T(8,128)} async-done(((f32[128,2048]{1,0:T(8,128)}), f32[32,2048]{1,0:T(8,128)}) %reduce-scatter.10.cloned.1.call-update) | async-done | bytes 262160
  158.5 0.0 reduce-scatter.12.cloned.1.call-update
  158.5 0.0 all-gather.2.cloned.1.call-start
  158.6 0.8 dynamic_slice.3
  159.3 0.1 broadcast_add_fusion
  159.4 16.6 %reduce-scatter.12.cloned.1.call-done = f32[16,2048]{1,0:T(8,128)} async-done(((f32[32,2048]{1,0:T(8,128)}), f32[16,2048]{1,0:T(8,128)}) %reduce-scatter.12.cloned.1.call-update) | async-done | bytes 131088
  176.0 1.2 copy.18
  177.2 0.3 fusion
  177.6 1.0 copy.11
  178.5 0.0 all-gather.2.cloned.1.call-update
  178.6 84.0 %all-gather.2.cloned.1.call-done = f32[1024,2048]{1,0:T(8,128)} async-done(((f32[16,2048]{1,0:T(8,128)}), f32[1024,2048]{1,0:T(8,128)}) %all-gather.2.cloned.1.call-update) | async-done | bytes 8388624 | tf_op jit(solution)/shard_map/all_gather | solution.py:81
  262.6 7.8 %convolution_bitcast_fusion.1 = f32[64,2048]{1,0:T(8,128)S(1)} fusion(f32[1024,2048]{1,0:T(8,128)} %all-gather.2.cloned.1.call-done, f32[64,1024]{1,0:T(8,128)S(1)} %copy-done.1), kind=kOutput, calls=%fused_computation.1 | convolution fusion | flops 1610612736 | bytes 9175040 | tf_op jit(solution)/shard_map/dot_general | solution.py:79
  270.4 0.4 reshape.45
  270.7 0.0 copy-done.2
  270.7 1.0 fusion.4
  271.8 0.2 copy.26
  271.9 12.8 %all_to_all.11 = f32[4,64,512]{2,1,0:T(8,128)S(1)} all-to-all(f32[4,64,512]{2,1,0:T(8,128)S(1)} %bitcast.39), channel_id=1, replica_groups=mesh['gz_0'=8,'gz_1'=4,'gz_2'=2,'col'=4] {'col'}, dimensions={0} | all-to-all | bytes 1048576 | tf_op jit(solution)/shard_map/all_to_all | solution.py:44
  284.8 1.8 fusion.8
  (11 shorter events, 0.1 us)
Async XLA Ops:
  6.5 1.2 copy-start
  6.5 125.7 %reduce-scatter.8.cloned.1.call-start = ((), (), s32[]{:S(2)}) async-start(), calls=%async_computation.5 | async-start | bytes 9437184 | tf_op jit(solution)/shard_map/reduce_scatter | solution.py:32
  35.1 123.4 %copy-start.3 = (f32[512]{0:T(512)S(1)}, f32[512]{0:T(512)}, u32[]{:S(2)}) copy-start(f32[512]{0:T(512)} %param.13) | copy-start | bytes 6148
  35.1 124.2 %copy-start.4 = (f32[4]{0:T(128)S(1)}, f32[4]{0:T(128)}, u32[]{:S(2)}) copy-start(f32[4]{0:T(128)} %param.12) | copy-start | bytes 52
  35.1 227.5 %copy-start.1 = (f32[64,1024]{1,0:T(8,128)S(1)}, f32[64,1024]{1,0:T(8,128)}, u32[]{:S(2)}) copy-start(f32[64,1024]{1,0:T(8,128)} %param.8) | copy-start | bytes 786436
  35.1 123.3 %reduce-scatter.10.cloned.1.call-start = ((), (), s32[]{:S(2)}) async-start(), calls=%async_computation.7 | async-start | bytes 1310720
  134.8 136.0 %copy-start.2 = (f32[4,4]{1,0:T(4,128)S(1)}, f32[4,4]{1,0:T(4,128)}, u32[]{:S(2)}) copy-start(f32[4,4]{1,0:T(4,128)} %param.9) | copy-start | bytes 196
  134.8 41.2 %reduce-scatter.12.cloned.1.call-start = ((), (), s32[]{:S(2)}) async-start(), calls=%async_computation.8 | async-start | bytes 393216
  158.5 104.1 %all-gather.2.cloned.1.call-start = ((), (), s32[]{:S(2)}) async-start(), calls=%async_computation.6 | async-start | bytes 8519680 | tf_op jit(solution)/shard_map/all_gather | solution.py:81
Sparse Core Ops, SparseCore 0:
  35.3 96.9 reduce-scatter.7
  134.9 23.4 reduce-scatter.9
  160.9 14.9 reduce-scatter.11
  178.7 83.8 all-gather.1
where the time goes:
time: 293 us
  waiting for transfers between devices  221 us (75%)
  blocking collectives  26.3 us (9%)
  matrix products  24.3 us (8%)
  between operations  13.3 us (5%)
  local copies, waits for them, and re-layouts  7.47 us (3%)
    reduce_scatter x1, waiting for transfers between devices, own_rows(): subtotal = lax.psum_scatter(subtotal, axis, scatter_dimension=0, tiled=True)  97.1 us
    all_gather x1, waiting for transfers between devices, shards(): lax.all_gather(scaled, GZ, axis=0, tiled=True)  84 us
    unnamed x6, waiting for transfers between devices  40.2 us
    all_to_all x1, blocking collectives, sent_to_all(): lax.all_to_all(jnp.broadcast_to(value[None], (devices, *value.shape)), ax...  13.4 us
    all_to_all x1, blocking collectives, sum_at_owner(): lax.all_to_all(cut_along(value, dim, devices), axis, 0, 0, tiled=True)  12.8 us
    dot_general x1, matrix products, lead_product(): lax.dot_general(left_side, right_side, (((0,), (0,)), ((), ())), precisio...  10 us
    dot_general x1, matrix products, shards(): jnp.dot(z_vectors, lax.all_gather(scaled, GZ, axis=0, tiled=True), precis...  7.81 us
  transfers between devices with their start and end apart: 4, of which 4 were waited for; matrix products, arithmetic and copies ran while one was open for 0% of the time, Pallas kernels for 0%

commit v1 on v0

v1 whole, which is shorter than its diff:
```python
import functools

import jax
import jax.numpy as jnp
from jax import lax
from jax.experimental import pallas as pl
from jax.experimental.pallas import tpu as pltpu
from jax.sharding import Mesh
from jax.sharding import PartitionSpec as P

NZ, NX, NC, NY = 8, 4, 2, 4
CH = 4
EXACT = lax.Precision.HIGHEST
MESH = pl.DeviceIdType.MESH


def dot(a, b):
    return lax.dot_general(
        a, b, (((1,), (0,)), ((), ())), precision=EXACT, preferred_element_type=jnp.float32
    )


def dot_nt(a, b):
    return lax.dot_general(
        a, b, (((1,), (1,)), ((), ())), precision=EXACT, preferred_element_type=jnp.float32
    )


def swap_blocks(parts):
    shape = parts[0].shape
    block = lax.broadcasted_iota(jnp.int32, shape, len(shape) - 1) // 32
    out = []
    for q in range(4):
        total = parts[q] if False else None
        for m in range(4):
            shift = 32 * ((m - q) % 4)
            moved = parts[m] if shift == 0 else pltpu.roll(parts[m], shift, len(shape) - 1)
            total = moved if total is None else jnp.where(block == m, moved, total)
        out.append(total)
    return out


def kernel(
    src, zv, yv, zval, xv, xval, yval, out,
    zg, fp, fg, ft, cs, cr, st, ba, bp, br, op, orr,
    zs_s, zs_r, zd_s, zd_r, fa_s, fa_r, fy_s, fy_r,
    cs_s, cs_r, st_s, st_r, by_s, by_r, oz_s, oz_r,
):
    z = lax.axis_index("z")
    x = lax.axis_index("x")
    c = lax.axis_index("c")
    y = lax.axis_index("y")
    pc = 1 - c
    kw = zv.shape[1] // CH
    waits = []

    def send(src_ref, dst_ref, s_sem, r_sem, dev):
        cp = pltpu.make_async_remote_copy(
            src_ref=src_ref, dst_ref=dst_ref, send_sem=s_sem, recv_sem=r_sem,
            device_id=dev, device_id_type=MESH,
        )
        cp.start()
        waits.append(cp)

    def await_recv(ref, sem):
        pltpu.make_async_remote_copy(
            src_ref=ref, dst_ref=ref, send_sem=sem, recv_sem=sem,
            device_id={"c": pc}, device_id_type=MESH,
        ).wait_recv()

    def zmod(k):
        return lax.rem(z + k + NZ, NZ)

    barrier = pltpu.get_barrier_semaphore()
    pl.semaphore_signal(barrier, inc=1, device_id={"c": pc}, device_id_type=MESH)
    for k in range(1, NZ):
        pl.semaphore_signal(barrier, inc=1, device_id={"z": zmod(k)}, device_id_type=MESH)
        pl.semaphore_signal(barrier, inc=1, device_id={"z": zmod(k), "c": pc}, device_id_type=MESH)
    for k in range(1, NX):
        pl.semaphore_signal(barrier, inc=1, device_id={"x": lax.rem(x + k, NX)}, device_id_type=MESH)
    for k in range(1, NY):
        pl.semaphore_signal(barrier, inc=1, device_id={"y": lax.rem(y + k, NY)}, device_id_type=MESH)

    along = dot(src[...], yv[...])
    for g in range(4):
        v = along[:, 128 * g : 128 * (g + 1)]
        pieces = swap_blocks([v[16 * m : 16 * (m + 1)] for m in range(4)])
        for q in range(4):
            fp[4 * g + q] = pieces[q]
    zg[c, z] = zv[...]
    fg[y, c, z] = fp[2 * z + c]

    pl.semaphore_wait(barrier, 1 + 2 * (NZ - 1) + (NX - 1) + (NY - 1))

    for k in (4, 3, 5, 2, 6, 1, 7):
        zz = zmod(k)
        for o in range(NC):
            cc = c if o == 0 else pc
            send(fp.at[2 * zz + cc], fg.at[y, c, z], fa_s.at[o, k], fa_r.at[o, k], {"z": zz, "c": cc})
    send(fp.at[2 * z + pc], fg.at[y, c, z], fa_s.at[1, 0], fa_r.at[1, 0], {"c": pc})

    def cols(ch):
        return pl.ds(ch * kw, kw)

    def ring_on(ch, s, way):
        zz = zmod(-s * way)
        block = zv.at[:, cols(ch)] if s == 0 else zg.at[c, zz, :, cols(ch)]
        w = 0 if way == 1 else 1
        send(block, zg.at[c, zz, :, cols(ch)], zs_s.at[w, s, ch], zs_r.at[w, s + 1, ch], {"z": zmod(way)})

    def to_partner(ch, s, way):
        zz = zmod(-s * way)
        block = zv.at[:, cols(ch)] if s == 0 else zg.at[c, zz, :, cols(ch)]
        w = 0 if way == 1 else 1
        send(block, zg.at[c, zz, :, cols(ch)], zd_s.at[w, s, ch], zd_r.at[w, s, ch], {"c": pc})

    def own(ch):
        ring_on(ch, 0, 1)
        ring_on(ch, 0, -1)
        to_partner(ch, 0, 1)

    def arrival(s, ch):
        for way in (1, -1):
            w = 0 if way == 1 else 1
            if s == NZ // 2 and (ch % 2 == 0) != (way == 1):
                continue
            await_recv(zg.at[c, zmod(-s * way), :, cols(ch)], zs_r.at[w, s, ch])
            if s + 1 < NZ // 2 or (s + 1 == NZ // 2 and (ch % 2 == 0) == (way == 1)):
                ring_on(ch, s, way)
            to_partner(ch, s, way)

    def partner_arrivals(ch):
        await_recv(zg.at[pc, z, :, cols(ch)], zd_r.at[0, 0, ch])
        for s in range(1, NZ // 2 + 1):
            for way in (1, -1):
                w = 0 if way == 1 else 1
                if s == NZ // 2 and (ch % 2 == 0) != (way == 1):
                    continue
                await_recv(zg.at[pc, zmod(-s * way), :, cols(ch)], zd_r.at[w, s, ch])

    def f_over_y():
        for k in range(1, NZ):
            zz = zmod(-k)
            for o in range(NC):
                cc = c if o == 0 else pc
                await_recv(fg.at[y, cc, zz], fa_r.at[o, k])
        await_recv(fg.at[y, pc, z], fa_r.at[1, 0])
        for k in (2, 1, 3):
            send(fg.at[y], fg.at[y], fy_s.at[k], fy_r.at[k], {"y": lax.rem(y + k, NY)})

    def f_turned():
        for k in range(1, NY):
            await_recv(fg.at[lax.rem(y - k + NY, NY)], fy_r.at[k])
        for pair in range(NC * NZ // 2):
            rows = []
            for b in (2 * pair, 2 * pair + 1):
                rows += swap_blocks([fg[p, b // NZ, b % NZ] for p in range(NY)])
            ft[:, 128 * pair : 128 * (pair + 1)] = jnp.concatenate(rows, axis=0).T

    def z_chunk(ch):
        return zg[:, :, :, ch * kw : (ch + 1) * kw].reshape(NC * NZ * 64, kw)

    def coefficients(ch):
        partner_arrivals(ch)
        part = dot(ft[...], z_chunk(ch))
        cs[ch] = part.reshape(4, NX, 8, kw)
        for k in (2, 1, 3):
            xx = lax.rem(x + k, NX)
            send(cs.at[ch, :, xx], cr.at[ch, k], cs_s.at[ch, k], cs_r.at[ch, k], {"x": xx})

    def scale(ch):
        total = cs[ch, :, x]
        for k in range(1, NX):
            await_recv(cr.at[ch, k], cs_r.at[ch, k])
            total = total + cr[ch, k]
        base = (2 * z + c) * 32 + 8 * x
        row = lax.broadcasted_iota(jnp.int32, (8, kw), 0)
        yvals = jnp.zeros((8, kw), jnp.float32)
        for t in range(8):
            yvals = jnp.where(row == t, yval[base + t], yvals)
        zy = yvals + zval[:, pl.ds(pl.multiple_of(y * zv.shape[1] + ch * kw, 128), kw)]
        scaled = []
        for i in range(4):
            mode = xv[0, i] * total[0]
            for p in range(1, 4):
                mode = mode + xv[p, i] * total[p]
            scaled.append(mode / (zy + xval[i]))
        for p in range(4):
            back = xv[p, 0] * scaled[0]
            for i in range(1, 4):
                back = back + xv[p, i] * scaled[i]
            st[ch, p, x] = back
        for k in (2, 1, 3):
            send(st.at[ch, :, x], st.at[ch, :, x], st_s.at[ch, k], st_r.at[ch, k], {"x": lax.rem(x + k, NX)})

    def scaled_all(ch):
        for k in range(1, NX):
            await_recv(st.at[ch, :, lax.rem(x - k + NX, NX)], st_r.at[ch, k])

    def back_z(ch):
        scaled_all(ch)
        part = dot_nt(z_chunk(ch), st[ch].reshape(128, kw))
        if ch == 0:
            ba[...] = part
        else:
            ba[...] += part

    own(0)
    own(1)
    arrival(1, 0)
    arrival(1, 1)
    f_over_y()
    arrival(2, 0)
    own(2)
    arrival(2, 1)
    own(3)
    arrival(3, 0)
    arrival(3, 1)
    arrival(1, 2)
    arrival(1, 3)
    f_turned()
    arrival(4, 0)
    arrival(4, 1)
    arrival(2, 2)
    arrival(2, 3)
    coefficients(0)
    coefficients(1)
    arrival(3, 2)
    arrival(3, 3)
    scale(0)
    scale(1)
    arrival(4, 2)
    arrival(4, 3)
    coefficients(2)
    back_z(0)
    coefficients(3)
    back_z(1)
    scale(2)
    scale(3)
    back_z(2)
    back_z(3)

    half = NZ // 2
    for cc in range(NC):
        for h in range(2):
            for b in range(half):
                at = (cc * NZ + h * half + b) * 64
                pieces = swap_blocks([ba[at + 16 * m : at + 16 * (m + 1), :] for m in range(4)])
                for p in range(NY):
                    bp[p, cc, h * half + b] = pieces[p]
            for k in (2, 1, 3):
                yy = lax.rem(y + k, NY)
                send(
                    bp.at[yy, cc, pl.ds(h * half, half)], br.at[k, cc, pl.ds(h * half, half)],
                    by_s.at[cc, h, k], by_r.at[cc, h, k], {"y": yy},
                )
    for cc in range(NC):
        for h in range(2):
            part = pl.ds(h * half, half)
            total = bp[y, cc, part]
            for k in range(1, NY):
                await_recv(br.at[k, cc, part], by_r.at[cc, h, k])
                total = total + br[k, cc, part]
            op[cc, part] = total
    for k in (4, 3, 5, 2, 6, 1, 7):
        zz = zmod(k)
        for o in range(NC):
            cc = c if o == 0 else pc
            send(op.at[cc, zz], orr.at[2 * z + c], oz_s.at[o, k], oz_r.at[o, k], {"z": zz, "c": cc})
    send(op.at[pc, z], orr.at[2 * z + c], oz_s.at[1, 0], oz_r.at[1, 0], {"c": pc})
    orr[2 * z + c] = op[c, z]
    for k in range(1, NZ):
        zz = zmod(-k)
        for o in range(NC):
            cc = c if o == 0 else pc
            await_recv(orr.at[2 * zz + cc], oz_r.at[o, k])
    await_recv(orr.at[2 * z + pc], oz_r.at[1, 0])
    lanes = []
    for g in range(4):
        lanes.append(jnp.concatenate(swap_blocks([orr[4 * g + q] for q in range(4)]), axis=0))
    out[...] = dot_nt(jnp.concatenate(lanes, axis=1), yv[...])

    for cp in waits:
        cp.wait_send()


def shards(source, z_vectors, x_vectors, y_vectors, z_values, x_values, y_values):
    f32 = jnp.float32
    dma = pltpu.SemaphoreType.DMA
    vmem = pl.BlockSpec(memory_space=pltpu.VMEM)
    smem = pl.BlockSpec(memory_space=pltpu.SMEM)
    kw = z_vectors.shape[1] // CH
    return pl.pallas_call(
        kernel,
        out_shape=jax.ShapeDtypeStruct(source.shape, f32),
        in_specs=[vmem, vmem, vmem, vmem, smem, smem, smem],
        out_specs=vmem,
        scratch_shapes=[
            pltpu.VMEM((NC, NZ, 64, z_vectors.shape[1]), f32),
            pltpu.VMEM((16, 16, 128), f32),
            pltpu.VMEM((NY, NC, NZ, 16, 128), f32),
            pltpu.VMEM((128, 1024), f32),
            pltpu.VMEM((CH, 4, NX, 8, kw), f32),
            pltpu.VMEM((CH, NX, 4, 8, kw), f32),
            pltpu.VMEM((CH, 4, NX, 8, kw), f32),
            pltpu.VMEM((1024, 128), f32),
            pltpu.VMEM((NY, NC, NZ, 16, 128), f32),
            pltpu.VMEM((NY, NC, NZ, 16, 128), f32),
            pltpu.VMEM((NC, NZ, 16, 128), f32),
            pltpu.VMEM((16, 16, 128), f32),
            dma((2, 5, CH)), dma((2, 5, CH)), dma((2, 5, CH)), dma((2, 5, CH)),
            dma((2, NZ)), dma((2, NZ)), dma((NY,)), dma((NY,)),
            dma((CH, NX)), dma((CH, NX)), dma((CH, NX)), dma((CH, NX)),
            dma((2, 2, NY)), dma((2, 2, NY)), dma((2, NZ)), dma((2, NZ)),
        ],
        compiler_params=pltpu.CompilerParams(
            collective_id=0, has_side_effects=True, vmem_limit_bytes=48 * 1024 * 1024
        ),
    )(source, z_vectors, y_vectors, z_values.reshape(1, -1), x_vectors, x_values, y_values)


def solution(mesh):
    torus = Mesh(mesh.devices.reshape(NZ, NX, NC, NY), ("z", "x", "c", "y"))
    rows = ("z", "x", "c")
    return jax.shard_map(
        shards,
        mesh=torus,
        in_specs=(P(rows, "y"), P(rows, "y"), P(), P(), P(), P(), P()),
        out_specs=P(rows, "y"),
        check_vma=False,
    )
```

time: 293 us -> 79.3 us (0.27)
  waiting for transfers between devices: 221 us -> 0 us
  Pallas kernels: 0 us -> 72.6 us
  blocking collectives: 26.3 us -> 0 us
  matrix products: 24.3 us -> 0 us
  between operations: 13.3 us -> 0.02 us
    reduce_scatter x1 -> x0, waiting for transfers between devices: 97.1 us -> none  [own_rows(): subtotal = lax.psum_scatter(subtotal, axis, scatter_dimension=0, tiled=True)]
    all_gather x1 -> x0, waiting for transfers between devices: 84 us -> none  [shards(): lax.all_gather(scaled, GZ, axis=0, tiled=True)]
    pallas_call x0 -> x1, Pallas kernels: none -> 72.6 us  [shards(): pl.pallas_call(kernel, out_shape=jax.ShapeDtypeStruct(source.shape, f32),...]
    unnamed x6 -> x0, waiting for transfers between devices: 40.2 us -> none
    all_to_all x2 -> x0, blocking collectives: 26.3 us -> none  [the longest x1 13.4 us: sent_to_all(): lax.all_to_all(jnp.broadcast_to(value[None], (devices, *value.shape)), ax...]
    dot_general x6 -> x0, matrix products: 24.3 us -> none  [the longest x1 10 us: lead_product(): lax.dot_general(left_side, right_side, (((0,), (0,)), ((), ())), precisio...]
  transfers between devices with their start and end apart: 4 -> 0, of which waited for: 4 -> 0; matrix products, arithmetic and copies ran while one was open for 0% -> 0% of each run, Pallas kernels for 0% -> 0%
where the time goes in v1:
time: 79.3 us; the launch traced here: 79.1 us
  Pallas kernels  72.6 us (92%)
  local copies, waits for them, and re-layouts  6.47 us (8%)
    pallas_call x1, Pallas kernels, shards(): pl.pallas_call(kernel, out_shape=jax.ShapeDtypeStruct(source.shape, f32),...  72.6 us
    unnamed x15, local copies, waits for them, and re-layouts  6.47 us

profile of v1, /device:TPU:1, one launch (start us, length us, event | category | flops | bytes accessed | tf_op | source)
XLA Modules:
  0.0 79.1 jit_solution(11515721313718732927)
XLA Ops:
  0.0 0.0 copy-start.6
  0.0 0.7 copy-done.6
  0.7 0.0 copy-start
  0.7 1.2 %copy-done = f32[512,512]{1,0:T(8,128)S(1)} copy-done((f32[512,512]{1,0:T(8,128)S(1)}, f32[512,512]{1,0:T(8,128)}, u32[]{:S(2)}) %copy-start) | copy-done | bytes 1048600
  1.9 0.0 copy-start.1
  1.9 0.9 %copy-done.1 = f32[64,1024]{1,0:T(8,128)S(1)} copy-done((f32[64,1024]{1,0:T(8,128)S(1)}, f32[64,1024]{1,0:T(8,128)}, u32[]{:S(2)}) %copy-start.1) | copy-done | bytes 262168
  2.8 0.0 copy-start.2
  2.8 0.9 %copy-done.2 = f32[64,512]{1,0:T(8,128)S(1)} copy-done((f32[64,512]{1,0:T(8,128)S(1)}, f32[64,512]{1,0:T(8,128)}, u32[]{:S(2)}) %copy-start.2) | copy-done | bytes 131096
  3.7 0.0 copy-start.3
  3.7 0.7 copy-done.3
  4.5 0.0 copy-start.4
  4.5 0.7 copy-done.4
  5.1 0.0 copy-start.5
  5.1 0.7 copy-done.5
  5.8 72.6 %shard_map.73 = f32[64,512]{1,0:T(8,128)S(1)} custom-call(f32[64,512]{1,0:T(8,128)S(1)} %copy-done.2, f32[64,1024]{1,0:T(8,128)S(1)} %copy-done.1, f32[512,512]{1,0:T(8,128)S(1)} %copy-done, f32[1,4096]{1,0:T(1,128)S(1)} %bitcast.1, f32[4,4]{1,0:T(4,128)S(1)} %copy-done.4, f32[4]{0:T(128)S(1)} %copy-done.6, f32[512]{0:T(512)S(1)} %copy-done.5), custom_call_target="tpu_custom_call" | custom-call | tf_op jit(solution)/shard_map/pallas_call | solution.py:293
  78.4 0.7 copy.9
Async XLA Ops:
  0.0 0.7 copy-start.6
  0.7 1.2 %copy-start = (f32[512,512]{1,0:T(8,128)S(1)}, f32[512,512]{1,0:T(8,128)}, u32[]{:S(2)}) copy-start(f32[512,512]{1,0:T(8,128)} %yv.1) | copy-start | bytes 3145732
  1.9 0.9 %copy-start.1 = (f32[64,1024]{1,0:T(8,128)S(1)}, f32[64,1024]{1,0:T(8,128)}, u32[]{:S(2)}) copy-start(f32[64,1024]{1,0:T(8,128)} %zv.1) | copy-start | bytes 786436
  2.8 0.9 %copy-start.2 = (f32[64,512]{1,0:T(8,128)S(1)}, f32[64,512]{1,0:T(8,128)}, u32[]{:S(2)}) copy-start(f32[64,512]{1,0:T(8,128)} %src.1) | copy-start | bytes 393220
  3.7 0.7 copy-start.3
  4.5 0.7 copy-start.4
  5.1 0.7 copy-start.5

commit v2 on v0

v2 whole, which is shorter than its diff:
```python
import jax
import jax.numpy as jnp
from jax import lax
from jax.experimental import pallas as pl
from jax.experimental.pallas import tpu as pltpu
from jax.sharding import Mesh
from jax.sharding import PartitionSpec as P

NZ, NX, NC, NY = 8, 4, 2, 4
MESH = pl.DeviceIdType.MESH
WIDTHS = (128, 256, 128, 128, 256, 128)
N = len(WIDTHS)
LAST = 3
STARTS = tuple(sum(WIDTHS[:ch]) for ch in range(N))
GROUPS = ((4, 3), (5, 2), (6, 1), (7, 0))


def dot_exact(a, b):
    return lax.dot_general(
        a, b, (((1,), (0,)), ((), ())),
        precision=lax.Precision.HIGHEST, preferred_element_type=jnp.float32,
    )


def dot(a, b, b_dim=0):
    return lax.dot_general(a, b, (((1,), (b_dim,)), ((), ())), preferred_element_type=jnp.float32)


def halves(value):
    high = value.astype(jnp.bfloat16)
    return high, (value - high.astype(jnp.float32)).astype(jnp.bfloat16)


def swap_blocks(parts):
    shape = parts[0].shape
    block = lax.broadcasted_iota(jnp.int32, shape, 1) // 32
    out = []
    for q in range(4):
        total = None
        for m in range(4):
            shift = 32 * ((m - q) % 4)
            moved = parts[m] if shift == 0 else pltpu.roll(parts[m], shift, 1)
            total = moved if total is None else jnp.where(block == m, moved, total)
        out.append(total)
    return out


def kernel(
    src_h, zv_h, yv_h, zval_h, xv_h, xval_h, yval_h, out,
    src, zv, yv, zval, xv, xval, yval, in_s,
    zg, zh, zl, yth, ytl, fp, fg, fts, cs, cr, st, ba, bp, br, op, orr,
    zs_s, zs_r, zd_s, zd_r, fa_s, fa_r, fy_s, fy_r,
    cs_s, cs_r, st_s, st_r, by_s, by_r, oz_s, oz_r,
):
    z = lax.axis_index("z")
    x = lax.axis_index("x")
    c = lax.axis_index("c")
    y = lax.axis_index("y")
    pc = 1 - c

    def send(src_ref, dst_ref, s_sem, r_sem, dev):
        pltpu.make_async_remote_copy(
            src_ref=src_ref, dst_ref=dst_ref, send_sem=s_sem, recv_sem=r_sem,
            device_id=dev, device_id_type=MESH,
        ).start()

    def sized(ref, sem):
        return pltpu.make_async_remote_copy(
            src_ref=ref, dst_ref=ref, send_sem=sem, recv_sem=sem,
            device_id={"c": pc}, device_id_type=MESH,
        )

    def received(ref, sem):
        sized(ref, sem).wait_recv()

    def sent(ref, sem):
        sized(ref, sem).wait_send()

    def zmod(k):
        return lax.rem(z + k + NZ, NZ)

    def core(o):
        return c if o == 0 else pc

    def cols(ch):
        return pl.ds(STARTS[ch], WIDTHS[ch])

    def load(n):
        pairs = [(zv_h, zv), (src_h, src), (yv_h, yv), (zval_h, zval), (xv_h, xv), (xval_h, xval), (yval_h, yval)]
        return pltpu.make_async_copy(*pairs[n], in_s.at[n])

    def start():
        for n in range(7):
            load(n).start()
        barrier = pltpu.get_barrier_semaphore()

        def greet(dev):
            pl.semaphore_signal(barrier, inc=1, device_id=dev, device_id_type=MESH)

        for k in (4, 3, 5, 2, 6, 1, 7):
            greet({"z": zmod(k)})
            greet({"z": zmod(k), "c": pc})
        for k in range(1, NX):
            greet({"x": lax.rem(x + k, NX)})
        for k in range(1, NY):
            greet({"y": lax.rem(y + k, NY)})
        greet({"c": pc})

    def along_y():
        load(1).wait()
        load(2).wait()
        along = dot_exact(src[...], yv[...])
        for g in range(4):
            v = along[:, 128 * g : 128 * (g + 1)]
            pieces = swap_blocks([v[16 * m : 16 * (m + 1)] for m in range(4)])
            for q in range(4):
                fp[4 * g + q] = pieces[q]
        fg[y, c, z] = fp[2 * z + c]

    def meet():
        load(0).wait()
        pl.semaphore_wait(pltpu.get_barrier_semaphore(), 1 + 2 * (NZ - 1) + (NX - 1) + (NY - 1))

    def pass_on(ch, s, way):
        slot = zmod(-s * way)
        block = zv.at[:, cols(ch)] if s == 0 else zg.at[c, slot, :, cols(ch)]
        if s < NZ // 2 - 1 or (s == NZ // 2 - 1 and (ch % 2 == 0) == (way == 1)):
            send(block, zg.at[c, slot, :, cols(ch)], zs_s, zs_r.at[s, ch], {"z": zmod(way)})
        if s > 0 or way == 1:
            send(block, zg.at[c, slot, :, cols(ch)], zd_s, zd_r.at[ch], {"c": pc})

    def own(ch):
        pass_on(ch, 0, 1)
        pass_on(ch, 0, -1)

    def arr(s, ch):
        ways = (1, -1) if s < NZ // 2 else ((1,) if ch % 2 == 0 else (-1,))
        received(zg.at[c, pl.ds(0, len(ways)), :, cols(ch)], zs_r.at[s - 1, ch])
        for way in ways:
            pass_on(ch, s, way)

    def prepare():
        zg[c, z] = zv[...]
        for n in range(3, 7):
            load(n).wait()
        high, low = halves(yv[...].T)
        yth[...] = high
        ytl[...] = low

    def a2a():
        for k in (4, 3, 5, 2, 6, 1, 7):
            for o in range(NC):
                dev = {"z": zmod(k), "c": core(o)}
                send(fp.at[2 * zmod(k) + core(o)], fg.at[y, c, z], fa_s, fa_r, dev)
        send(fp.at[2 * z + pc], fg.at[y, c, z], fa_s, fa_r, {"c": pc})

    def fy():
        received(fp.at[pl.ds(0, 15)], fa_r)
        for k in (2, 1, 3):
            send(fg.at[y], fg.at[y], fy_s, fy_r, {"y": lax.rem(y + k, NY)})

    def ft():
        received(fg.at[pl.ds(0, NY - 1)], fy_r)
        for pair in range(NC * NZ // 2):
            rows = []
            for b in (2 * pair, 2 * pair + 1):
                rows += swap_blocks([fg[p, b // NZ, b % NZ] for p in range(NY)])
            high, low = halves(jnp.concatenate(rows, axis=0).T)
            fts[0:128, 128 * pair : 128 * (pair + 1)] = high
            fts[128:256, 128 * pair : 128 * (pair + 1)] = low

    def C(ch):
        lo, hi = STARTS[ch], STARTS[ch] + WIDTHS[ch]
        received(zg.at[pc, :, :, cols(ch)], zd_r.at[ch])
        high, low = halves(zg[:, :, :, lo:hi].reshape(NC * NZ * 64, WIDTHS[ch]))
        zh[:, lo:hi] = high
        zl[:, lo:hi] = low
        both = dot(fts[...], high)
        part = both[:128] + both[128:] + dot(fts[:128], low)
        cs[:, :, :, lo:hi] = part.reshape(4, NX, 8, WIDTHS[ch])
        for k in (2, 1, 3):
            xx = lax.rem(x + k, NX)
            send(cs.at[:, xx, :, cols(ch)], cr.at[k - 1, :, :, cols(ch)], cs_s, cs_r.at[ch], {"x": xx})

    def S(ch):
        lo, hi = STARTS[ch], STARTS[ch] + WIDTHS[ch]
        received(cr.at[:, :, :, cols(ch)], cs_r.at[ch])
        base = (2 * z + c) * 32 + 8 * x
        row = lax.broadcasted_iota(jnp.int32, (8, WIDTHS[ch]), 0)
        yvals = jnp.zeros((8, WIDTHS[ch]), jnp.float32)
        for t in range(8):
            yvals = jnp.where(row == t, yval[base + t], yvals)
        zy = yvals + zval[:, pl.ds(pl.multiple_of(y * zv.shape[1] + lo, 128), WIDTHS[ch])]
        total = [
            cs[p, x, :, lo:hi] + cr[0, p, :, lo:hi] + cr[1, p, :, lo:hi] + cr[2, p, :, lo:hi] for p in range(4)
        ]
        scaled = []
        for i in range(4):
            mode = xv[0, i] * total[0]
            for p in range(1, 4):
                mode = mode + xv[p, i] * total[p]
            scaled.append(mode / (zy + xval[i]))
        for p in range(4):
            back = xv[p, 0] * scaled[0]
            for i in range(1, 4):
                back = back + xv[p, i] * scaled[i]
            st[p, x, :, lo:hi] = back
        for k in (2, 1, 3):
            piece = st.at[:, x, :, cols(ch)]
            send(piece, piece, st_s, st_r.at[ch], {"x": lax.rem(x + k, NX)})

    def modes_back(high, low, ch):
        lo, hi = STARTS[ch], STARTS[ch] + WIDTHS[ch]
        s_high, s_low = halves(st[:, :, :, lo:hi].reshape(128, WIDTHS[ch]))
        both = dot(high, jnp.concatenate([s_high, s_low], axis=0), 1)
        return both[:, :128] + both[:, 128:] + dot(low, s_high, 1)

    def B(ch):
        lo, hi = STARTS[ch], STARTS[ch] + WIDTHS[ch]
        received(st.at[:, pl.ds(0, NX - 1), :, cols(ch)], st_r.at[ch])
        if ch == LAST:
            return
        part = modes_back(zh[:, lo:hi], zl[:, lo:hi], ch)
        if ch == 0:
            ba[...] = part
        else:
            ba[...] += part

    def blocks(g):
        return [(k, o, (core(o) * NZ + zmod(k)) * 64) for k in GROUPS[g] for o in range(NC)]

    def over_y(g):
        lo, hi = STARTS[LAST], STARTS[LAST] + WIDTHS[LAST]

        def rows(ref, a, b):
            return jnp.concatenate(
                [ref[pl.ds(pl.multiple_of(at, 64), 64), a:b] for _, _, at in blocks(g)], axis=0
            )

        total = rows(ba, 0, 128) + modes_back(rows(zh, lo, hi), rows(zl, lo, hi), LAST)
        for n in range(4):
            pieces = swap_blocks([total[64 * n + 16 * m : 64 * n + 16 * (m + 1)] for m in range(4)])
            for p in range(NY):
                bp[p, g, n] = pieces[p]
        for k in (2, 1, 3):
            yy = lax.rem(y + k, NY)
            send(bp.at[yy, g], br.at[k - 1, g], by_s, by_r.at[g], {"y": yy})

    def leave(g):
        received(br.at[:, g], by_r.at[g])
        op[g] = bp[y, g] + br[0, g] + br[1, g] + br[2, g]
        for n, (k, o, _) in enumerate(blocks(g)):
            if k == 0 and o == 0:
                orr[2 * z + c] = op[g, n]
            else:
                send(op.at[g, n], orr.at[2 * z + c], oz_s, oz_r, {"z": zmod(k), "c": core(o)})

    def finish():
        received(orr.at[pl.ds(0, 15)], oz_r)
        lanes = []
        for g in range(4):
            lanes.append(jnp.concatenate(swap_blocks([orr[4 * g + q] for q in range(4)]), axis=0))
        high, low = halves(jnp.concatenate(lanes, axis=1))
        both = dot(jnp.concatenate([high, low], axis=0), yth[...])
        out[...] = both[:64] + both[64:] + dot(high, ytl[...])

    def drain():
        sent(zg.at[0, pl.ds(0, NZ - 1)], zs_s)
        sent(zg.at[0], zd_s)
        sent(fp.at[pl.ds(0, 15)], fa_s)
        sent(fg.at[pl.ds(0, NY - 1)], fy_s)
        sent(cr, cs_s)
        sent(st.at[:, pl.ds(0, NX - 1)], st_s)
        sent(br, by_s)
        sent(orr.at[pl.ds(0, 15)], oz_s)

    plan = [
        (start,), (along_y,), (meet,),
        (own, 0), (own, 1), (prepare,), (a2a,), (arr, 1, 0), (own, 4), (arr, 1, 1), (arr, 2, 0), (fy,),
        (own, 2), (arr, 1, 4), (arr, 2, 1), (own, 5), (arr, 3, 0), (own, 3), (arr, 1, 2), (arr, 2, 4),
        (arr, 3, 1), (arr, 1, 5), (ft,), (arr, 4, 0), (arr, 1, 3), (arr, 2, 2), (C, 0), (arr, 3, 4),
        (arr, 4, 1), (arr, 2, 5), (C, 1), (arr, 2, 3), (arr, 3, 2), (S, 0), (arr, 4, 4), (arr, 3, 5), (C, 4),
        (arr, 3, 3), (arr, 4, 2), (S, 1), (arr, 4, 5), (C, 2), (B, 0), (arr, 4, 3), (C, 5), (C, 3), (S, 4),
        (B, 1), (S, 2), (S, 5), (S, 3), (B, 4), (B, 2), (B, 5), (B, 3),
        (over_y, 0), (over_y, 1), (over_y, 2), (over_y, 3),
        (leave, 0), (leave, 1), (leave, 2), (leave, 3),
        (finish,), (drain,),
    ]
    for step, *args in plan:
        with jax.named_scope("_".join([step.__name__, *map(str, args)])):
            step(*args)


def shards(source, z_vectors, x_vectors, y_vectors, z_values, x_values, y_values):
    f32, bf16 = jnp.float32, jnp.bfloat16
    vmem, smem, dma = pltpu.VMEM, pltpu.SMEM, pltpu.SemaphoreType.DMA
    modes = z_vectors.shape[1]
    one = dma(())
    return pl.pallas_call(
        kernel,
        out_shape=jax.ShapeDtypeStruct(source.shape, f32),
        in_specs=[pl.BlockSpec(memory_space=pl.ANY)] * 7,
        out_specs=pl.BlockSpec(memory_space=pltpu.VMEM),
        scratch_shapes=[
            vmem(source.shape, f32),
            vmem(z_vectors.shape, f32),
            vmem(y_vectors.shape, f32),
            vmem((1, z_values.shape[0]), f32),
            smem(x_vectors.shape, f32),
            smem(x_values.shape, f32),
            smem(y_values.shape, f32),
            dma((7,)),
            vmem((NC, NZ, 64, modes), f32),
            vmem((1024, modes), bf16),
            vmem((1024, modes), bf16),
            vmem((512, 512), bf16),
            vmem((512, 512), bf16),
            vmem((16, 16, 128), f32),
            vmem((NY, NC, NZ, 16, 128), f32),
            vmem((256, 1024), bf16),
            vmem((4, NX, 8, modes), f32),
            vmem((NX - 1, 4, 8, modes), f32),
            vmem((4, NX, 8, modes), f32),
            vmem((1024, 128), f32),
            vmem((NY, 4, 4, 16, 128), f32),
            vmem((NY - 1, 4, 4, 16, 128), f32),
            vmem((4, 4, 16, 128), f32),
            vmem((16, 16, 128), f32),
            one, dma((4, N)), one, dma((N,)), one, one, one, one,
            one, dma((N,)), one, dma((N,)), one, dma((4,)), one, one,
        ],
        compiler_params=pltpu.CompilerParams(
            collective_id=0, has_side_effects=True, vmem_limit_bytes=67_043_328
        ),
    )(source, z_vectors, y_vectors, z_values.reshape(1, -1), x_vectors, x_values, y_values)


def solution(mesh):
    torus = Mesh(mesh.devices.reshape(NZ, NX, NC, NY), ("z", "x", "c", "y"))
    rows = ("z", "x", "c")
    return jax.shard_map(
        shards,
        mesh=torus,
        in_specs=(P(rows, "y"), P(rows, "y"), P(), P(), P(), P(), P()),
        out_specs=P(rows, "y"),
        check_vma=False,
    )
```

time: 293 us -> 63 us (0.22)
  waiting for transfers between devices: 221 us -> 0 us
  Pallas kernels: 0 us -> 61.3 us
  blocking collectives: 26.3 us -> 0 us
  matrix products: 24.3 us -> 0 us
  between operations: 13.3 us -> 0.01 us
  local copies, waits for them, and re-layouts: 7.47 us -> 1.57 us
    reduce_scatter x1 -> x0, waiting for transfers between devices: 97.1 us -> none  [own_rows(): subtotal = lax.psum_scatter(subtotal, axis, scatter_dimension=0, tiled=True)]
    all_gather x1 -> x0, waiting for transfers between devices: 84 us -> none  [shards(): lax.all_gather(scaled, GZ, axis=0, tiled=True)]
    pallas_call x0 -> x1, Pallas kernels: none -> 61.3 us  [shards(): pl.pallas_call(kernel, out_shape=jax.ShapeDtypeStruct(source.shape, f32),...]
    unnamed x6 -> x0, waiting for transfers between devices: 40.2 us -> none
    all_to_all x2 -> x0, blocking collectives: 26.3 us -> none  [the longest x1 13.4 us: sent_to_all(): lax.all_to_all(jnp.broadcast_to(value[None], (devices, *value.shape)), ax...]
    dot_general x6 -> x0, matrix products: 24.3 us -> none  [the longest x1 10 us: lead_product(): lax.dot_general(left_side, right_side, (((0,), (0,)), ((), ())), precisio...]
    unnamed x15 -> x1, local copies, waits for them, and re-layouts: 5.17 us -> 1.57 us
  transfers between devices with their start and end apart: 4 -> 0, of which waited for: 4 -> 0; matrix products, arithmetic and copies ran while one was open for 0% -> 0% of each run, Pallas kernels for 0% -> 0%
where the time goes in v2:
time: 63 us; the launch traced here: 62.9 us
  Pallas kernels  61.3 us (97%)
  local copies, waits for them, and re-layouts  1.57 us (2%)
    pallas_call x1, Pallas kernels, shards(): pl.pallas_call(kernel, out_shape=jax.ShapeDtypeStruct(source.shape, f32),...  61.3 us
    unnamed x1, local copies, waits for them, and re-layouts  1.57 us

profile of v2, /device:TPU:1, one launch (start us, length us, event | category | flops | bytes accessed | tf_op | source)
XLA Modules:
  0.0 62.9 jit_solution(2581916775078443109)
XLA Ops:
  0.0 61.3 %shard_map.73 = f32[64,512]{1,0:T(8,128)} custom-call(f32[64,512]{1,0:T(8,128)} %src_h.1, f32[64,1024]{1,0:T(8,128)} %zv_h.1, f32[512,512]{1,0:T(8,128)} %yv_h.1, f32[1,4096]{1,0:T(1,128)} %bitcast.1, f32[4,4]{1,0:T(4,128)} %xv_h.1, f32[4]{0:T(128)} %xval_h.1, f32[512]{0:T(512)} %yval_h.1), custom_call_target="tpu_custom_call" | custom-call | tf_op jit(solution)/shard_map/pallas_call | solution.py:299
  61.3 1.6 %copy.9 = f32[64,512]{1,0:T(8,128)} copy(f32[64,512]{1,0:T(8,128)} %shard_map.73) | data formatting | bytes 262144

commit v3 on v2

--- a/solution.py
+++ b/solution.py
@@ -50,7 +50,7 @@
     src, zv, yv, zval, xv, xval, yval, in_s,
     zg, zh, zl, yth, ytl, fp, fg, fts, cs, cr, st, ba, bp, br, op, orr,
     zs_s, zs_r, zd_s, zd_r, fa_s, fa_r, fy_s, fy_r,
-    cs_s, cs_r, st_s, st_r, by_s, by_r, oz_s, oz_r,
+    cs_s, cs_r, st_s, st_r, by_s, by_r, oz_s, oz_r, zi, xi, yi, pi,
 ):
     z = lax.axis_index("z")
     x = lax.axis_index("x")
@@ -79,6 +79,15 @@
     def zmod(k):
         return lax.rem(z + k + NZ, NZ)
 
+    def xmod(k):
+        return lax.rem(x + k + NX, NX)
+
+    def ymod(k):
+        return lax.rem(y + k + NY, NY)
+
+    def tell(sem, dev):
+        pl.semaphore_signal(sem, inc=1, device_id=dev, device_id_type=MESH)
+
     def core(o):
         return c if o == 0 else pc
 
@@ -92,19 +101,10 @@
     def start():
         for n in range(7):
             load(n).start()
-        barrier = pltpu.get_barrier_semaphore()
-
-        def greet(dev):
-            pl.semaphore_signal(barrier, inc=1, device_id=dev, device_id_type=MESH)
-
-        for k in (4, 3, 5, 2, 6, 1, 7):
-            greet({"z": zmod(k)})
-            greet({"z": zmod(k), "c": pc})
-        for k in range(1, NX):
-            greet({"x": lax.rem(x + k, NX)})
-        for k in range(1, NY):
-            greet({"y": lax.rem(y + k, NY)})
-        greet({"c": pc})
+        for dev in (
+            {"z": zmod(1)}, {"z": zmod(-1)}, {"x": xmod(1)}, {"x": xmod(-1)}, {"y": ymod(1)}, {"y": ymod(-1)}, {"c": pc}
+        ):
+            tell(pltpu.get_barrier_semaphore(), dev)
 
     def along_y():
         load(1).wait()
@@ -119,7 +119,25 @@
 
     def meet():
         load(0).wait()
-        pl.semaphore_wait(pltpu.get_barrier_semaphore(), 1 + 2 * (NZ - 1) + (NX - 1) + (NY - 1))
+        pl.semaphore_wait(pltpu.get_barrier_semaphore(), 7)
+        tell(zi.at[0, 0], {"z": zmod(1)})
+        tell(zi.at[1, 0], {"z": zmod(-1)})
+        tell(xi, {"x": xmod(-1)})
+        tell(yi, {"y": ymod(-1)})
+
+    def meet_far():
+        pl.semaphore_wait(zi.at[0, 0], 1)
+        tell(zi.at[0, 1], {"z": zmod(1)})
+        pl.semaphore_wait(zi.at[1, 0], 1)
+        tell(zi.at[1, 1], {"z": zmod(-1)})
+        pl.semaphore_wait(zi.at[0, 1], 1)
+        tell(zi.at[0, 2], {"z": zmod(1)})
+        pl.semaphore_wait(zi.at[1, 1], 1)
+        pl.semaphore_wait(xi, 1)
+        pl.semaphore_wait(yi, 1)
+        pl.semaphore_wait(zi.at[0, 2], 1)
+        tell(pi, {"c": pc})
+        pl.semaphore_wait(pi, 1)
 
     def pass_on(ch, s, way):
         slot = zmod(-s * way)
@@ -157,7 +175,7 @@
     def fy():
         received(fp.at[pl.ds(0, 15)], fa_r)
         for k in (2, 1, 3):
-            send(fg.at[y], fg.at[y], fy_s, fy_r, {"y": lax.rem(y + k, NY)})
+            send(fg.at[y], fg.at[y], fy_s, fy_r, {"y": ymod(k)})
 
     def ft():
         received(fg.at[pl.ds(0, NY - 1)], fy_r)
@@ -179,7 +197,7 @@
         part = both[:128] + both[128:] + dot(fts[:128], low)
         cs[:, :, :, lo:hi] = part.reshape(4, NX, 8, WIDTHS[ch])
         for k in (2, 1, 3):
-            xx = lax.rem(x + k, NX)
+            xx = xmod(k)
             send(cs.at[:, xx, :, cols(ch)], cr.at[k - 1, :, :, cols(ch)], cs_s, cs_r.at[ch], {"x": xx})
 
     def S(ch):
@@ -207,7 +225,7 @@
             st[p, x, :, lo:hi] = back
         for k in (2, 1, 3):
             piece = st.at[:, x, :, cols(ch)]
-            send(piece, piece, st_s, st_r.at[ch], {"x": lax.rem(x + k, NX)})
+            send(piece, piece, st_s, st_r.at[ch], {"x": xmod(k)})
 
     def modes_back(high, low, ch):
         lo, hi = STARTS[ch], STARTS[ch] + WIDTHS[ch]
@@ -243,7 +261,7 @@
             for p in range(NY):
                 bp[p, g, n] = pieces[p]
         for k in (2, 1, 3):
-            yy = lax.rem(y + k, NY)
+            yy = ymod(k)
             send(bp.at[yy, g], br.at[k - 1, g], by_s, by_r.at[g], {"y": yy})
 
     def leave(g):
@@ -253,16 +271,20 @@
             if k == 0 and o == 0:
                 orr[2 * z + c] = op[g, n]
             else:
-                send(op.at[g, n], orr.at[2 * z + c], oz_s, oz_r, {"z": zmod(k), "c": core(o)})
-
-    def finish():
-        received(orr.at[pl.ds(0, 15)], oz_r)
-        lanes = []
-        for g in range(4):
-            lanes.append(jnp.concatenate(swap_blocks([orr[4 * g + q] for q in range(4)]), axis=0))
-        high, low = halves(jnp.concatenate(lanes, axis=1))
-        both = dot(jnp.concatenate([high, low], axis=0), yth[...])
-        out[...] = both[:64] + both[64:] + dot(high, ytl[...])
+                send(op.at[g, n], orr.at[2 * z + c], oz_s, oz_r.at[g], {"z": zmod(k), "c": core(o)})
+
+    def last(g):
+        received(orr.at[pl.ds(0, 3 if g == 3 else 4)], oz_r.at[g])
+        near = [zmod(-k) for k in GROUPS[g]]
+        parts = swap_blocks([orr[2 * zz + cc] for zz in near for cc in range(NC)])
+        high, low = halves(jnp.concatenate(parts, axis=0))
+
+        def rows(ref):
+            return jnp.concatenate([ref[pl.ds(pl.multiple_of(64 * zz, 64), 64), :] for zz in near], axis=0)
+
+        both = dot(jnp.concatenate([high, low], axis=0), rows(yth))
+        part = both[:64] + both[64:] + dot(high, rows(ytl))
+        out[...] = part if g == 0 else out[...] + part
 
     def drain():
         sent(zg.at[0, pl.ds(0, NZ - 1)], zs_s)
@@ -275,16 +297,16 @@
         sent(orr.at[pl.ds(0, 15)], oz_s)
 
     plan = [
-        (start,), (along_y,), (meet,),
-        (own, 0), (own, 1), (prepare,), (a2a,), (arr, 1, 0), (own, 4), (arr, 1, 1), (arr, 2, 0), (fy,),
-        (own, 2), (arr, 1, 4), (arr, 2, 1), (own, 5), (arr, 3, 0), (own, 3), (arr, 1, 2), (arr, 2, 4),
-        (arr, 3, 1), (arr, 1, 5), (ft,), (arr, 4, 0), (arr, 1, 3), (arr, 2, 2), (C, 0), (arr, 3, 4),
-        (arr, 4, 1), (arr, 2, 5), (C, 1), (arr, 2, 3), (arr, 3, 2), (S, 0), (arr, 4, 4), (arr, 3, 5), (C, 4),
-        (arr, 3, 3), (arr, 4, 2), (S, 1), (arr, 4, 5), (C, 2), (B, 0), (arr, 4, 3), (C, 5), (C, 3), (S, 4),
-        (B, 1), (S, 2), (S, 5), (S, 3), (B, 4), (B, 2), (B, 5), (B, 3),
+        (start,), (meet,),
+        (own, 0), (own, 1), (own, 4), (along_y,), (meet_far,), (a2a,), (prepare,), (arr, 1, 0), (arr, 1, 1),
+        (own, 2), (arr, 1, 4), (arr, 2, 0), (fy,), (arr, 2, 1), (own, 5), (own, 3), (arr, 1, 2), (arr, 2, 4),
+        (arr, 3, 0), (arr, 3, 1), (arr, 1, 5), (arr, 1, 3), (arr, 2, 2), (ft,), (arr, 3, 4), (arr, 4, 0),
+        (arr, 4, 1), (C, 0), (arr, 2, 5), (C, 1), (arr, 2, 3), (arr, 3, 2), (arr, 4, 4), (arr, 3, 5), (C, 4),
+        (arr, 3, 3), (S, 0), (arr, 4, 2), (S, 1), (arr, 4, 5), (C, 2), (arr, 4, 3), (C, 5), (C, 3), (S, 4),
+        (B, 0), (B, 1), (S, 2), (S, 5), (S, 3), (B, 4), (B, 2), (B, 5), (B, 3),
         (over_y, 0), (over_y, 1), (over_y, 2), (over_y, 3),
         (leave, 0), (leave, 1), (leave, 2), (leave, 3),
-        (finish,), (drain,),
+        (last, 0), (last, 1), (last, 2), (last, 3), (drain,),
     ]
     for step, *args in plan:
         with jax.named_scope("_".join([step.__name__, *map(str, args)])):
@@ -296,10 +318,11 @@
     vmem, smem, dma = pltpu.VMEM, pltpu.SMEM, pltpu.SemaphoreType.DMA
     modes = z_vectors.shape[1]
     one = dma(())
+    told = pltpu.SemaphoreType.REGULAR
     return pl.pallas_call(
         kernel,
         out_shape=jax.ShapeDtypeStruct(source.shape, f32),
-        in_specs=[pl.BlockSpec(memory_space=pl.ANY)] * 7,
+        in_specs=[pl.BlockSpec(memory_space=pltpu.HBM)] * 7,
         out_specs=pl.BlockSpec(memory_space=pltpu.VMEM),
         scratch_shapes=[
             vmem(source.shape, f32),
@@ -327,12 +350,16 @@
             vmem((4, 4, 16, 128), f32),
             vmem((16, 16, 128), f32),
             one, dma((4, N)), one, dma((N,)), one, one, one, one,
-            one, dma((N,)), one, dma((N,)), one, dma((4,)), one, one,
+            one, dma((N,)), one, dma((N,)), one, dma((4,)), one, dma((4,)),
+            told((2, 3)), told(()), told(()), told(()),
         ],
         compiler_params=pltpu.CompilerParams(
-            collective_id=0, has_side_effects=True, vmem_limit_bytes=67_043_328
+            collective_id=0, has_side_effects=True, vmem_limit_bytes=32 * 1024 * 1024
         ),
-    )(source, z_vectors, y_vectors, z_values.reshape(1, -1), x_vectors, x_values, y_values)
+    )(*[
+        pltpu.with_memory_space_constraint(a, pltpu.HBM)
+        for a in (source, z_vectors, y_vectors, z_values.reshape(1, -1), x_vectors, x_values, y_values)
+    ])
 
 
 def solution(mesh):

time: 63 us -> 59.7 us (0.948)
  Pallas kernels: 61.3 us -> 58.9 us
  local copies, waits for them, and re-layouts: 1.57 us -> 0.66 us
    pallas_call x1, Pallas kernels: 61.3 us -> 58.9 us  [shards(): pl.pallas_call(kernel, out_shape=jax.ShapeDtypeStruct(source.shape, f32),...]
    unnamed x1, local copies, waits for them, and re-layouts: 1.57 us -> 0.66 us
where the time goes in v3:
time: 59.7 us; the launch traced here: 59.6 us
  Pallas kernels  58.9 us (99%)
  local copies, waits for them, and re-layouts  0.66 us (1%)
    pallas_call x1, Pallas kernels, shards(): pl.pallas_call(kernel, out_shape=jax.ShapeDtypeStruct(source.shape, f32),...  58.9 us

profile of v3, /device:TPU:1, one launch (start us, length us, event | category | flops | bytes accessed | tf_op | source)
XLA Modules:
  0.0 59.6 jit_solution(15807569985119980808)
XLA Ops:
  0.0 58.9 %shard_map.73 = f32[64,512]{1,0:T(8,128)S(1)} custom-call(f32[64,512]{1,0:T(8,128)} %src_h.1, f32[64,1024]{1,0:T(8,128)} %zv_h.1, f32[512,512]{1,0:T(8,128)} %yv_h.1, f32[1,4096]{1,0:T(1,128)} %bitcast.1, f32[4,4]{1,0:T(4,128)} %xv_h.1, f32[4]{0:T(128)} %xval_h.1, f32[512]{0:T(512)} %yval_h.1), custom_call_target="tpu_custom_call" | custom-call | tf_op jit(solution)/shard_map/pallas_call | solution.py:322
  58.9 0.7 %copy.9 = f32[64,512]{1,0:T(8,128)} copy(f32[64,512]{1,0:T(8,128)S(1)} %shard_map.73) | data formatting | bytes 262144

commit v4 on v3

--- a/solution.py
+++ b/solution.py
@@ -8,11 +8,11 @@
 
 NZ, NX, NC, NY = 8, 4, 2, 4
 MESH = pl.DeviceIdType.MESH
-WIDTHS = (128, 256, 128, 128, 256, 128)
+WIDTHS = (128, 128, 128, 128, 128, 128, 128, 128)
 N = len(WIDTHS)
-LAST = 3
+FIRST, LAST = 0, 2
 STARTS = tuple(sum(WIDTHS[:ch]) for ch in range(N))
-GROUPS = ((4, 3), (5, 2), (6, 1), (7, 0))
+FAR_FIRST = (4, 3, 5, 2, 6, 1, 7, 0)
 
 
 def dot_exact(a, b):
@@ -99,12 +99,13 @@
         return pltpu.make_async_copy(*pairs[n], in_s.at[n])
 
     def start():
-        for n in range(7):
+        load(0).start()
+        for way in (1, -1):
+            for dev in ({"z": zmod(way)}, {"z": zmod(way), "c": pc}, {"x": xmod(way)}, {"y": ymod(way)}):
+                tell(pltpu.get_barrier_semaphore(), dev)
+        tell(pltpu.get_barrier_semaphore(), {"c": pc})
+        for n in range(1, 7):
             load(n).start()
-        for dev in (
-            {"z": zmod(1)}, {"z": zmod(-1)}, {"x": xmod(1)}, {"x": xmod(-1)}, {"y": ymod(1)}, {"y": ymod(-1)}, {"c": pc}
-        ):
-            tell(pltpu.get_barrier_semaphore(), dev)
 
     def along_y():
         load(1).wait()
@@ -119,25 +120,23 @@
 
     def meet():
         load(0).wait()
-        pl.semaphore_wait(pltpu.get_barrier_semaphore(), 7)
+        pl.semaphore_wait(pltpu.get_barrier_semaphore(), 9)
         tell(zi.at[0, 0], {"z": zmod(1)})
         tell(zi.at[1, 0], {"z": zmod(-1)})
         tell(xi, {"x": xmod(-1)})
         tell(yi, {"y": ymod(-1)})
 
+    def meet_second():
+        pl.semaphore_wait(zi.at[0, 0], 1)
+        pl.semaphore_wait(zi.at[1, 0], 1)
+        tell(zi.at[0, 1], {"z": zmod(2)})
+        tell(zi.at[1, 1], {"z": zmod(-2)})
+
     def meet_far():
-        pl.semaphore_wait(zi.at[0, 0], 1)
-        tell(zi.at[0, 1], {"z": zmod(1)})
-        pl.semaphore_wait(zi.at[1, 0], 1)
-        tell(zi.at[1, 1], {"z": zmod(-1)})
         pl.semaphore_wait(zi.at[0, 1], 1)
-        tell(zi.at[0, 2], {"z": zmod(1)})
         pl.semaphore_wait(zi.at[1, 1], 1)
         pl.semaphore_wait(xi, 1)
         pl.semaphore_wait(yi, 1)
-        pl.semaphore_wait(zi.at[0, 2], 1)
-        tell(pi, {"c": pc})
-        pl.semaphore_wait(pi, 1)
 
     def pass_on(ch, s, way):
         slot = zmod(-s * way)
@@ -165,17 +164,26 @@
         yth[...] = high
         ytl[...] = low
 
-    def a2a():
-        for k in (4, 3, 5, 2, 6, 1, 7):
+    def a2(part):
+        if part == 0:
+            along_y()
+        if part == 1:
+            meet_second()
+        if part == 2:
+            meet_far()
+        for k in ((1, -1), (2, -2), (4, 3, -3))[part]:
             for o in range(NC):
                 dev = {"z": zmod(k), "c": core(o)}
-                send(fp.at[2 * zmod(k) + core(o)], fg.at[y, c, z], fa_s, fa_r, dev)
-        send(fp.at[2 * z + pc], fg.at[y, c, z], fa_s, fa_r, {"c": pc})
-
-    def fy():
-        received(fp.at[pl.ds(0, 15)], fa_r)
+                send(fp.at[2 * zmod(k) + core(o)], fg.at[y, c, z], fa_s, fa_r.at[part // 2], dev)
+        if part == 0:
+            send(fp.at[2 * z + pc], fg.at[y, c, z], fa_s, fa_r.at[0], {"c": pc})
+
+    def fy(part):
+        received(fp.at[pl.ds(0, 9 if part == 0 else 6)], fa_r.at[part])
         for k in (2, 1, 3):
-            send(fg.at[y], fg.at[y], fy_s, fy_r, {"y": ymod(k)})
+            for d in ((0, 1, -1, 2, -2), (3, -3, 4))[part]:
+                piece = fg.at[y, :, zmod(d)]
+                send(piece, piece, fy_s, fy_r, {"y": ymod(k)})
 
     def ft():
         received(fg.at[pl.ds(0, NY - 1)], fy_r)
@@ -239,13 +247,13 @@
         if ch == LAST:
             return
         part = modes_back(zh[:, lo:hi], zl[:, lo:hi], ch)
-        if ch == 0:
+        if ch == FIRST:
             ba[...] = part
         else:
             ba[...] += part
 
     def blocks(g):
-        return [(k, o, (core(o) * NZ + zmod(k)) * 64) for k in GROUPS[g] for o in range(NC)]
+        return [(k, o, (core(o) * NZ + zmod(k)) * 64) for k in FAR_FIRST[2 * g : 2 * g + 2] for o in range(NC)]
 
     def over_y(g):
         lo, hi = STARTS[LAST], STARTS[LAST] + WIDTHS[LAST]
@@ -275,7 +283,7 @@
 
     def last(g):
         received(orr.at[pl.ds(0, 3 if g == 3 else 4)], oz_r.at[g])
-        near = [zmod(-k) for k in GROUPS[g]]
+        near = [zmod(-k) for k in FAR_FIRST[2 * g : 2 * g + 2]]
         parts = swap_blocks([orr[2 * zz + cc] for zz in near for cc in range(NC)])
         high, low = halves(jnp.concatenate(parts, axis=0))
 
@@ -298,14 +306,15 @@
 
     plan = [
         (start,), (meet,),
-        (own, 0), (own, 1), (own, 4), (along_y,), (meet_far,), (a2a,), (prepare,), (arr, 1, 0), (arr, 1, 1),
-        (own, 2), (arr, 1, 4), (arr, 2, 0), (fy,), (arr, 2, 1), (own, 5), (own, 3), (arr, 1, 2), (arr, 2, 4),
-        (arr, 3, 0), (arr, 3, 1), (arr, 1, 5), (arr, 1, 3), (arr, 2, 2), (ft,), (arr, 3, 4), (arr, 4, 0),
-        (arr, 4, 1), (C, 0), (arr, 2, 5), (C, 1), (arr, 2, 3), (arr, 3, 2), (arr, 4, 4), (arr, 3, 5), (C, 4),
-        (arr, 3, 3), (S, 0), (arr, 4, 2), (S, 1), (arr, 4, 5), (C, 2), (arr, 4, 3), (C, 5), (C, 3), (S, 4),
-        (B, 0), (B, 1), (S, 2), (S, 5), (S, 3), (B, 4), (B, 2), (B, 5), (B, 3),
-        (over_y, 0), (over_y, 1), (over_y, 2), (over_y, 3),
-        (leave, 0), (leave, 1), (leave, 2), (leave, 3),
+        (own, 0), (own, 3), (a2, 0), (a2, 1), (own, 5), (arr, 1, 0), (a2, 2), (prepare,), (arr, 1, 3),
+        (fy, 0), (arr, 1, 5), (arr, 2, 0), (own, 6), (own, 1), (arr, 2, 3), (own, 7), (arr, 2, 5), (own, 4),
+        (own, 2), (arr, 3, 0), (fy, 1), (arr, 1, 6), (arr, 1, 1), (arr, 3, 3), (arr, 1, 7), (arr, 3, 5),
+        (arr, 1, 4), (arr, 1, 2), (ft,), (arr, 4, 0), (arr, 2, 6), (arr, 2, 1), (arr, 4, 3), (C, 0),
+        (arr, 2, 7), (C, 3), (arr, 4, 5), (arr, 2, 4), (arr, 2, 2), (C, 5), (arr, 3, 6), (arr, 3, 1), (S, 0),
+        (arr, 3, 7), (S, 3), (arr, 3, 4), (arr, 3, 2), (arr, 4, 6), (S, 5), (arr, 4, 1), (C, 6), (arr, 4, 7),
+        (C, 1), (arr, 4, 4), (C, 7), (arr, 4, 2), (C, 4), (C, 2), (B, 0), (S, 6), (S, 1), (S, 7), (S, 4),
+        (S, 2), (B, 3), (B, 5), (B, 6), (B, 1), (B, 7), (B, 4), (B, 2),
+        *((over_y, g) for g in range(4)), *((leave, g) for g in range(4)),
         (last, 0), (last, 1), (last, 2), (last, 3), (drain,),
     ]
     for step, *args in plan:
@@ -349,9 +358,9 @@
             vmem((NY - 1, 4, 4, 16, 128), f32),
             vmem((4, 4, 16, 128), f32),
             vmem((16, 16, 128), f32),
-            one, dma((4, N)), one, dma((N,)), one, one, one, one,
+            one, dma((4, N)), one, dma((N,)), one, dma((2,)), one, one,
             one, dma((N,)), one, dma((N,)), one, dma((4,)), one, dma((4,)),
-            told((2, 3)), told(()), told(()), told(()),
+            told((2, 2)), told(()), told(()), told(()),
         ],
         compiler_params=pltpu.CompilerParams(
             collective_id=0, has_side_effects=True, vmem_limit_bytes=32 * 1024 * 1024

time: 59.7 us -> 58.4 us (0.978)
  Pallas kernels: 58.9 us -> 57.7 us
    pallas_call x1, Pallas kernels: 58.9 us -> 57.7 us  [shards(): pl.pallas_call(kernel, out_shape=jax.ShapeDtypeStruct(source.shape, f32),...]
where the time goes in v4:
time: 58.4 us; the launch traced here: 58.3 us
  Pallas kernels  57.7 us (99%)
  local copies, waits for them, and re-layouts  0.66 us (1%)
    pallas_call x1, Pallas kernels, shards(): pl.pallas_call(kernel, out_shape=jax.ShapeDtypeStruct(source.shape, f32),...  57.7 us

profile of v4, /device:TPU:1, one launch (start us, length us, event | category | flops | bytes accessed | tf_op | source)
XLA Modules:
  0.0 58.3 jit_solution(11743627744800324721)
XLA Ops:
  0.0 57.7 %shard_map.73 = f32[64,512]{1,0:T(8,128)S(1)} custom-call(f32[64,512]{1,0:T(8,128)} %src_h.1, f32[64,1024]{1,0:T(8,128)} %zv_h.1, f32[512,512]{1,0:T(8,128)} %yv_h.1, f32[1,4096]{1,0:T(1,128)} %bitcast.1, f32[4,4]{1,0:T(4,128)} %xv_h.1, f32[4]{0:T(128)} %xval_h.1, f32[512]{0:T(512)} %yval_h.1), custom_call_target="tpu_custom_call" | custom-call | tf_op jit(solution)/shard_map/pallas_call | solution.py:331
  57.7 0.7 %copy.9 = f32[64,512]{1,0:T(8,128)} copy(f32[64,512]{1,0:T(8,128)S(1)} %shard_map.73) | data formatting | bytes 262144

commit v5 on v4

--- a/solution.py
+++ b/solution.py
@@ -310,8 +310,8 @@
         (fy, 0), (arr, 1, 5), (arr, 2, 0), (own, 6), (own, 1), (arr, 2, 3), (own, 7), (arr, 2, 5), (own, 4),
         (own, 2), (arr, 3, 0), (fy, 1), (arr, 1, 6), (arr, 1, 1), (arr, 3, 3), (arr, 1, 7), (arr, 3, 5),
         (arr, 1, 4), (arr, 1, 2), (ft,), (arr, 4, 0), (arr, 2, 6), (arr, 2, 1), (arr, 4, 3), (C, 0),
-        (arr, 2, 7), (C, 3), (arr, 4, 5), (arr, 2, 4), (arr, 2, 2), (C, 5), (arr, 3, 6), (arr, 3, 1), (S, 0),
-        (arr, 3, 7), (S, 3), (arr, 3, 4), (arr, 3, 2), (arr, 4, 6), (S, 5), (arr, 4, 1), (C, 6), (arr, 4, 7),
+        (arr, 2, 7), (C, 3), (arr, 4, 5), (arr, 2, 4), (arr, 2, 2), (C, 5), (arr, 3, 6), (arr, 3, 1),
+        (arr, 3, 7),  (arr, 3, 4), (arr, 3, 2), (S, 0), (S, 3), (S, 5), (arr, 4, 6),  (arr, 4, 1), (C, 6), (arr, 4, 7),
         (C, 1), (arr, 4, 4), (C, 7), (arr, 4, 2), (C, 4), (C, 2), (B, 0), (S, 6), (S, 1), (S, 7), (S, 4),
         (S, 2), (B, 3), (B, 5), (B, 6), (B, 1), (B, 7), (B, 4), (B, 2),
         *((over_y, g) for g in range(4)), *((leave, g) for g in range(4)),

time: 58.4 us -> 58.4 us (level)
  no operation moved by 1% of the time
where the time goes in v5:
time: 58.4 us; the launch traced here: 58.3 us
  Pallas kernels  57.6 us (99%)
  local copies, waits for them, and re-layouts  0.66 us (1%)
    pallas_call x1, Pallas kernels, shards(): pl.pallas_call(kernel, out_shape=jax.ShapeDtypeStruct(source.shape, f32),...  57.6 us

profile of v5, /device:TPU:1, one launch (start us, length us, event | category | flops | bytes accessed | tf_op | source)
XLA Modules:
  0.0 58.3 jit_solution(3567511719545369218)
XLA Ops:
  0.0 57.6 %shard_map.73 = f32[64,512]{1,0:T(8,128)S(1)} custom-call(f32[64,512]{1,0:T(8,128)} %src_h.1, f32[64,1024]{1,0:T(8,128)} %zv_h.1, f32[512,512]{1,0:T(8,128)} %yv_h.1, f32[1,4096]{1,0:T(1,128)} %bitcast.1, f32[4,4]{1,0:T(4,128)} %xv_h.1, f32[4]{0:T(128)} %xval_h.1, f32[512]{0:T(512)} %yval_h.1), custom_call_target="tpu_custom_call" | custom-call | tf_op jit(solution)/shard_map/pallas_call | solution.py:331
  57.6 0.7 %copy.9 = f32[64,512]{1,0:T(8,128)} copy(f32[64,512]{1,0:T(8,128)S(1)} %shard_map.73) | data formatting | bytes 262144
